TPU v7x, 768 devices: a whole 4x8x12 slice. The times are simulated.
768 devices in a mesh: section: 16 (over x, y_hi, core), mp: 48 (over z, y_lo).
Axes of the slice: x: 4, y: 8 (y_hi: 2, y_lo: 4; y = y_hi * 4 + y_lo), z: 12, core: 2. Of those that a mesh axis runs over, the one named last changes fastest.
Arguments:
- encoder_input: bfloat16 [2304, 1024], P('section'), may hold values from -6 to 6
- input_gain: float32 [1024], replicated, may hold values from 0.1 to 1.9
- expand_weight: bfloat16 [1024, 49152], P(None, 'mp'), may hold values from -0.1875 to 0.1875
- reduce_weight: bfloat16 [49152, 1024], P('mp'), may hold values from -0.02734375 to 0.02734375
- final_gain: float32 [1024], replicated, may hold values from 0.1 to 1.9
- decoder_input: bfloat16 [4096, 1024], P('section'), may hold values from -6 to 6
- query_gain: float32 [1024], replicated, may hold values from 0.1 to 1.9
- query_weight: bfloat16 [1024, 12288], P(None, 'mp'), may hold values from -2 to 2
- key_weight: bfloat16 [1024, 12288], P(None, 'mp'), may hold values from -0.1875 to 0.1875
- value_weight: bfloat16 [1024, 12288], P(None, 'mp'), may hold values from -0.1875 to 0.1875
- mixing_weight: bfloat16 [12288, 1024], P('mp'), may hold values from -0.0546875 to 0.0546875
- output_gradient: bfloat16 [4096, 1024], P('section'), may hold values from -342 to 342
Outputs:
- memory: bfloat16 [2304, 1024], P(('section', 'mp'))
- memory_gradient: bfloat16 [2304, 1024], P(('section', 'mp'))
All inputs are finite; a program needn't handle non-finite values.
Results may differ from a plain program's by a relative error of at most 0.025.
The roundings to bfloat16 on the way count: a program that leaves them out, or rounds other values in their place, can miss the bound.
Values may be sent and summed in bfloat16 or wider, within the bound.
A program may use at most 64 MiB of HBM per device.

v0:
```python
import jax
import jax.numpy as jnp
from jax import lax
from jax.sharding import PartitionSpec as P

DK = 128


def cut_along(x, dim, length):
    before, after = (x.shape[:dim], x.shape[dim + 1 :])
    return jnp.moveaxis(x.reshape(*before, length, -1, *after), dim, 0)


def sum_at_owner(x, axis, dim):
    length = lax.axis_size(axis)
    pieces = lax.all_to_all(cut_along(x, dim, length), axis, 0, 0, tiled=True)
    return jnp.sum(pieces, axis=0)


def laid_out(pieces, dim):
    dims = list(pieces.shape[1:])
    dims[dim] *= pieces.shape[0]
    return jnp.moveaxis(pieces, 0, dim).reshape(dims)


def from_everyone(x, axis):
    length = lax.axis_size(axis)
    return lax.all_to_all(jnp.broadcast_to(x[None], (length, *x.shape)), axis, 0, 0, tiled=True)


def gather_directly(x, axis, dim):
    return laid_out(from_everyone(x, axis), dim)


def in_one_piece(arrays, axis, dim, along):
    both = jnp.concatenate(arrays, axis=along)
    filled, at, gathered = (lax.all_gather(both, axis, axis=dim, tiled=True), 0, [])
    for a in arrays:
        gathered.append(lax.slice_in_dim(filled, at, at + a.shape[along], axis=along))
        at += a.shape[along]
    return tuple(gathered)


def gathered_once(x, axis):
    leaves = jax.tree.leaves(x)
    order = sorted(range(len(leaves)), key=lambda k: -leaves[k].size)
    width = (1, *leaves[order[0]].shape)[-1]
    lines = [
        jnp.pad(leaves[k].reshape(-1), (0, -leaves[k].size % width)).reshape(-1, width)
        for k in order
    ]
    both, at, found = (from_everyone(jnp.concatenate(lines), axis), 0, {})
    for k, line in zip(order, lines):
        slab = both[:, at : at + len(line)].reshape(len(both), -1)
        found[k] = slab[:, : leaves[k].size].reshape(-1, *leaves[k].shape)
        at += len(line)
    numbers = iter(range(len(leaves)))
    return jax.tree.map(lambda _: found[next(numbers)], x)


def folded_in_pairs(pieces, combine):
    while len(jax.tree.leaves(pieces)[0]) > 1:
        pieces = jax.vmap(combine)(
            *(jax.tree.map(lambda part: part[side::2], pieces) for side in (0, 1))
        )
    return jax.tree.map(lambda part: part[0], pieces)


def merged(x, axis, combine):
    pieces = gathered_once(x, axis)
    return folded_in_pairs(pieces, combine)


def norm_rows(rows, gain):
    values = rows.astype(jnp.float32)
    return values * lax.rsqrt(jnp.mean(values * values, axis=-1, keepdims=True) + 1e-06) * gain


def combine(first, second):
    top = jnp.maximum(first[0], second[0])
    left = jnp.exp(first[0] - top)
    right = jnp.exp(second[0] - top)
    return (top, first[1] * left + second[1] * right, first[2] * left + second[2] * right)


def body(
    encoder_input,
    input_gain,
    expand_weight,
    reduce_weight,
    final_gain,
    decoder_input,
    query_gain,
    query_weight,
    key_weight,
    value_weight,
    mixing_weight,
    output_gradient,
):
    scale = DK ** (-0.5)
    heads = key_weight.shape[1] // DK
    width = heads * DK
    normed = norm_rows(encoder_input, input_gain).astype(jnp.bfloat16)
    hidden = jnp.maximum(
        jnp.dot(normed, expand_weight, preferred_element_type=jnp.float32), 0.0
    ).astype(jnp.bfloat16)
    partial_value = jnp.dot(hidden, reduce_weight, preferred_element_type=jnp.float32)
    share = encoder_input.shape[0] // lax.axis_size("mp")
    offset = lax.axis_index("mp") * share
    owned = sum_at_owner(partial_value, "mp", 0)
    own_input = lax.dynamic_slice_in_dim(encoder_input, offset, share, 0)
    memory_own = norm_rows(own_input.astype(jnp.float32) + owned, final_gain).astype(jnp.bfloat16)
    memory = gather_directly(memory_own, "mp", 0)
    keys = jnp.dot(memory, key_weight, preferred_element_type=jnp.float32).astype(jnp.bfloat16)
    values = jnp.dot(memory, value_weight, preferred_element_type=jnp.float32).astype(jnp.bfloat16)
    dec_normed = norm_rows(decoder_input, query_gain).astype(jnp.bfloat16)
    queries = jnp.dot(dec_normed, query_weight, preferred_element_type=jnp.float32).astype(
        jnp.bfloat16
    )
    head_grad = jnp.einsum(
        "qd,id->qi", output_gradient, mixing_weight, preferred_element_type=jnp.float32
    ).astype(jnp.bfloat16)
    all_queries, all_grads = in_one_piece((queries, head_grad), "section", 0, 1)
    query_heads = all_queries.reshape(all_queries.shape[0], heads, DK)
    grad_heads = all_grads.reshape(all_grads.shape[0], heads, DK)
    key_heads = keys.reshape(keys.shape[0], heads, DK)
    value_heads = values.reshape(values.shape[0], heads, DK)
    scores = (
        jnp.einsum("qhd,khd->hqk", query_heads, key_heads, preferred_element_type=jnp.float32)
        * scale
    )
    local_top = jnp.max(scores, axis=-1)
    weights = jnp.exp(scores - local_top[..., None])
    prob_grad = jnp.einsum(
        "qhd,khd->hqk", grad_heads, value_heads, preferred_element_type=jnp.float32
    )
    top, total, numer = merged(
        (local_top, jnp.sum(weights, axis=-1), jnp.sum(weights * prob_grad, axis=-1)),
        "section",
        combine,
    )
    probs = jnp.exp(scores - top[..., None]) / total[..., None]
    delta = (numer / total)[..., None]
    score_grad = (probs * (prob_grad - delta) * scale).astype(jnp.bfloat16)
    key_grad = (
        jnp.einsum("hqk,qhd->khd", score_grad, query_heads, preferred_element_type=jnp.float32)
        .reshape(keys.shape[0], width)
        .astype(jnp.bfloat16)
    )
    value_grad = (
        jnp.einsum(
            "hqk,qhd->khd",
            probs.astype(jnp.bfloat16),
            grad_heads,
            preferred_element_type=jnp.float32,
        )
        .reshape(keys.shape[0], width)
        .astype(jnp.bfloat16)
    )
    first = jnp.einsum("ki,di->kd", key_grad, key_weight, preferred_element_type=jnp.float32)
    second = jnp.einsum("ki,di->kd", value_grad, value_weight, preferred_element_type=jnp.float32)
    gradient = sum_at_owner(first + second, "mp", 0)
    return (memory_own, gradient.astype(jnp.bfloat16))


def solution(mesh):
    in_specs = (
        P("section", None),
        P(),
        P(None, "mp"),
        P("mp", None),
        P(),
        P("section", None),
        P(),
        P(None, "mp"),
        P(None, "mp"),
        P(None, "mp"),
        P("mp", None),
        P("section", None),
    )
    out_specs = (P(("section", "mp"), None), P(("section", "mp"), None))
    return jax.shard_map(body, mesh=mesh, in_specs=in_specs, out_specs=out_specs, check_vma=False)
```

profile of v0, /device:TPU:1, one launch (start us, length us, event | category | flops | bytes accessed | tf_op | source)
XLA Modules:
  0.0 239.8 jit_solution(5031861982969171919)
XLA Ops:
  7.2 0.0 copy-start
  7.2 0.0 copy-start.3
  7.2 0.0 copy-start.5
  7.2 0.0 all-gather.2.cloned.1.call-start
  7.2 1.4 fusion.18
  8.6 1.5 convolution_convert_fusion
  10.2 1.7 convolution_convert_fusion.1
  11.8 0.7 pad_maximum_fusion
  12.6 0.0 all-gather.2.cloned.1.call-update
  12.6 1.1 fusion.21
  13.7 0.0 copy-done
  13.7 0.0 copy-done.3
  13.7 0.0 copy-done.5
  13.8 0.0 copy-start.6
  13.8 0.0 copy-start.1
  13.8 2.5 %fusion.7 = f32[144,1024]{1,0:T(8,128)S(1)} fusion(bf16[1024,1024]{1,0:T(8,128)(2,1)S(1)} %copy-done, bf16[1024,1024]{1,0:T(8,128)(2,1)} %param.14, bf16[144,1024]{1,0:T(8,128)(2,1)S(1)} %copy-done.3, f32[1024]{0:T(1024)S(1)} %copy-done.5, f32[144]{0:T(256)S(1)} %add_rsqrt_fusion.1), kind=kOutput, calls=%fused_computation.16 | convolution fusion | flops 604864512 | bytes 5083712 | tf_op jit(solution)/shard_map/dot_general | solution.py:107
  16.3 1.1 reshape.76
  17.4 19.4 %all-to-all-start = ((f32[48,3,1024]{2,1,0:T(4,128)}), f32[48,3,1024]{2,1,0:T(4,128)S(1)}, u32[]{:S(2)}, u32[]{:S(2)}) async-start(f32[48,3,1024]{2,1,0:T(4,128)} %reshape.76), calls=%async_computation | async-start | bytes 1572864 | tf_op jit(solution)/shard_map/all_to_all | solution.py:16
  36.8 31.7 %all-to-all-done = f32[48,3,1024]{2,1,0:T(4,128)S(1)} async-done(((f32[48,3,1024]{2,1,0:T(4,128)}), f32[48,3,1024]{2,1,0:T(4,128)S(1)}, u32[]{:S(2)}, u32[]{:S(2)}) %all-to-all-start) | async-done | bytes 589856 | tf_op jit(solution)/shard_map/all_to_all | solution.py:16
  68.6 0.1 reduce_sum.64
  68.7 0.9 multiply_reduce_fusion.1
  69.6 0.0 copy-done.6
  69.6 0.8 multiply_convert_fusion.6
  70.5 0.0 copy-start.4
  70.5 0.1 broadcast_in_dim.4
  70.6 28.1 %all_to_all.20 = bf16[48,3,1024]{2,1,0:T(4,128)(2,1)S(1)} all-to-all(bf16[48,3,1024]{2,1,0:T(4,128)(2,1)S(1)} %broadcast_in_dim.4), channel_id=1, replica_groups=mesh['section'=16,'mp'=48] {'mp'}, dimensions={0} | all-to-all | bytes 589824 | tf_op jit(solution)/shard_map/all_to_all | solution.py:28
  98.7 0.2 reshape.78
  98.9 0.0 copy-done.1
  98.9 0.2 fusion.16
  99.2 1.3 fusion.15
  100.5 26.0 %all-gather.2.cloned.1.call-done = bf16[4096,512]{0,1:T(8,128)(2,1)} async-done(((bf16[256,512]{0,1:T(8,128)(2,1)}), bf16[4096,512]{0,1:T(8,128)(2,1)}) %all-gather.2.cloned.1.call-update) | async-done | bytes 4194320 | tf_op jit(solution)/shard_map/all_gather | solution.py:37
  126.5 2.5 %fusion.53 = (bf16[4096,256]{0,1:T(8,128)(2,1)S(1)}, bf16[4096,256]{0,1:T(8,128)(2,1)S(1)}) fusion(bf16[4096,512]{0,1:T(8,128)(2,1)} %all-gather.2.cloned.1.call-done), kind=kLoop, calls=%fused_computation.88 | loop fusion | bytes 8388608 | tf_op jit(solution)/shard_map/slice | solution.py:39
  129.0 0.0 copy-done.4
  129.0 0.8 fusion.55
  129.8 1.5 fusion
  131.4 0.2 broadcast_in_dim.5
  131.6 52.4 %all_to_all.21 = f32[16,6,4096]{2,1,0:T(8,128)S(1)} all-to-all(f32[16,6,4096]{2,1,0:T(8,128)S(1)} %broadcast_in_dim.5), channel_id=1, replica_groups=mesh['section'=16,'mp'=48] {'section'}, dimensions={0} | all-to-all | bytes 3145728 | tf_op jit(solution)/shard_map/all_to_all | solution.py:28
  184.0 0.8 fusion.54
  184.8 0.4 multiply_add_fusion
  185.2 0.4 multiply_add_fusion.1
  185.6 0.2 multiply_add_fusion.2
  185.8 0.2 multiply_add_fusion.3
  186.0 0.1 multiply_add_fusion.4
  186.1 0.1 multiply_add_fusion.5
  186.2 0.1 fusion.46
  186.3 1.0 fusion.12
  187.3 0.0 copy-start.2
  187.3 1.4 fusion.17
  188.7 0.0 copy-done.2
  188.7 0.3 fusion.36
  189.0 0.3 convolution_add_fusion
  189.3 1.1 reshape.82
  190.5 41.8 %all_to_all.22 = f32[48,3,1024]{2,1,0:T(4,128)S(1)} all-to-all(f32[48,3,1024]{2,1,0:T(4,128)} %reshape.82), channel_id=1, replica_groups=mesh['section'=16,'mp'=48] {'mp'}, dimensions={0} | all-to-all | bytes 1179648 | tf_op jit(solution)/shard_map/all_to_all | solution.py:16
  232.3 0.7 reduce_sum.69
  (5 shorter events, 0.1 us)
Async XLA Ops:
  7.2 6.6 %copy-start = (bf16[1024,1024]{1,0:T(8,128)(2,1)S(1)}, bf16[1024,1024]{1,0:T(8,128)(2,1)}, u32[]{:S(2)}) copy-start(bf16[1024,1024]{1,0:T(8,128)(2,1)} %param.15) | copy-start | bytes 6291460
  7.2 6.6 %copy-start.3 = (bf16[144,1024]{1,0:T(8,128)(2,1)S(1)}, bf16[144,1024]{1,0:T(8,128)(2,1)}, u32[]{:S(2)}) copy-start(bf16[144,1024]{1,0:T(8,128)(2,1)} %param.12) | copy-start | bytes 884740
  7.2 6.6 %copy-start.5 = (f32[1024]{0:T(1024)S(1)}, f32[1024]{0:T(1024)}, u32[]{:S(2)}) copy-start(f32[1024]{0:T(1024)} %param.13) | copy-start | bytes 12292
  7.2 119.3 %all-gather.2.cloned.1.call-start = ((), (), s32[]{:S(2)}) async-start(), calls=%async_computation.4 | async-start | bytes 4456448 | tf_op jit(solution)/shard_map/all_gather | solution.py:37
  13.8 55.9 %copy-start.6 = (f32[1024]{0:T(1024)S(1)}, f32[1024]{0:T(1024)}, u32[]{:S(2)}) copy-start(f32[1024]{0:T(1024)} %param.16) | copy-start | bytes 12292
  13.8 85.1 %copy-start.1 = (bf16[1024,256]{1,0:T(8,128)(2,1)S(1)}, bf16[1024,256]{1,0:T(8,128)(2,1)}, u32[]{:S(2)}) copy-start(bf16[1024,256]{1,0:T(8,128)(2,1)} %param.21) | copy-start | bytes 1572868
  17.4 51.2 %all-to-all-start = ((f32[48,3,1024]{2,1,0:T(4,128)}), f32[48,3,1024]{2,1,0:T(4,128)S(1)}, u32[]{:S(2)}, u32[]{:S(2)}) async-start(f32[48,3,1024]{2,1,0:T(4,128)} %reshape.76), calls=%async_computation | async-start | bytes 1572864 | tf_op jit(solution)/shard_map/all_to_all | solution.py:16
  70.5 58.5 %copy-start.4 = (bf16[3,1024]{1,0:T(4,128)(2,1)}, bf16[3,1024]{1,0:T(4,128)(2,1)S(1)}, u32[]{:S(2)}) copy-start(bf16[3,1024]{1,0:T(4,128)(2,1)S(1)} %multiply_convert_fusion.6) | copy-start | bytes 18436
  187.3 1.4 copy-start.2
Sparse Core Ops, SparseCore 0:
  12.7 113.7 all-gather.1
where the time goes:
time: 241 us; the launch traced here: 240 us
  blocking collectives  122 us (51%)
  waiting for transfers between devices  57.8 us (24%)
  starting transfers between devices  19.4 us (8%)
  between operations  14.3 us (6%)
  matrix products  12.5 us (5%)
  other arithmetic  7.33 us (3%)
  local copies, waits for them, and re-layouts  6.14 us (3%)
    all_to_all x2, blocking collectives, from_everyone(): lax.all_to_all(jnp.broadcast_to(x[None], (length, *x.shape)), axis, 0, 0,...  80.5 us
    all_to_all x1, blocking collectives, sum_at_owner(): pieces = lax.all_to_all(cut_along(x, dim, length), axis, 0, 0, tiled=True)  41.8 us
    all_to_all x1, waiting for transfers between devices, sum_at_owner(): pieces = lax.all_to_all(cut_along(x, dim, length), axis, 0, 0, tiled=True)  31.7 us
    all_gather x1, waiting for transfers between devices, in_one_piece(): lax.all_gather(both, axis, axis=dim, tiled=True)  26 us
    all_to_all x1, starting transfers between devices, sum_at_owner(): pieces = lax.all_to_all(cut_along(x, dim, length), axis, 0, 0, tiled=True)  19.4 us
  transfers between devices with their start and end apart: 2, of which 2 were waited for; matrix products, arithmetic and copies ran while one was open for 4% of the time, Pallas kernels for 0%

commit v1 on v0

v1 whole, which is shorter than its diff:
```python
import jax
import jax.numpy as jnp
from jax import lax
from jax.experimental import pallas as pl
from jax.experimental.pallas import tpu as pltpu
from jax.sharding import PartitionSpec as P

DK = 128
D = 1024
CHUNKS = D // 128
MP = 48
ROWS = 144
SHARE = ROWS // MP
PIECE = SHARE * CHUNKS
QROWS = 256
QALL = 4096
BLOCK = 512
BLOCKS = QALL // BLOCK
WIDTH = 2 * DK
SCALE = DK ** (-0.5)
BF = jnp.bfloat16
F32 = jnp.float32


def dot(a, b):
    return jnp.dot(a, b, preferred_element_type=F32)


def dot_t(a, b):
    return lax.dot_general(a, b, (((1,), (1,)), ((), ())), preferred_element_type=F32)


def norm_rows(rows, gain):
    values = rows.astype(F32)
    return values * lax.rsqrt(jnp.mean(values * values, axis=-1, keepdims=True) + 1e-06) * gain


def merge(a, b):
    top = jnp.maximum(a[0], b[0])
    left = jnp.exp(a[0] - top)
    right = jnp.exp(b[0] - top)
    return top, a[1] * left + b[1] * right, a[2] * left + b[2] * right


def kernel(
    x_hbm, ig_ref, we_hbm, wr_hbm, fg_ref, dec_hbm, qg_ref, wq_hbm, wk_hbm, wv_hbm, mix_hbm, og_hbm,
    mem_out, grad_out,
    x_v, we_v, wr_v, dec_v, wq_v, wk_v, wv_v, mix_v, og_v, load_sem,
    wide, stage, own, res, send, recv, send2, recv2, gath, mem,
    qg, wts, pgr, stats, got_d, mid, got_y, pair, got_x, fin,
    rs_s, rs_r, ag_s, ag_r, rs2_s, rs2_r,
    y_s, y_r, x_s, x_r, h_s, h_r, d_s, d_r,
    sd_s, sd_r, sy_s, sy_r, sx_s, sx_r, sf_s, sf_r,
):
    sec = lax.axis_index("section")
    me = lax.axis_index("mp")
    xi = sec // 4
    yi = (sec // 2) % 2
    core = sec % 2

    def section_of(dx, dy, dc):
        return (((xi + dx) % 4) * 2 + (yi + dy) % 2) * 2 + (core + dc) % 2

    ypeer, dpeer = section_of(0, 1, 0), section_of(0, 0, 1)
    right, left, across = section_of(1, 0, 0), section_of(3, 0, 0), section_of(2, 0, 0)

    def remote(src, dst, ss, rs, s, m):
        return pltpu.make_async_remote_copy(
            src_ref=src, dst_ref=dst, send_sem=ss, recv_sem=rs, device_id=(s, m),
            device_id_type=pl.DeviceIdType.MESH,
        )

    barrier = pltpu.get_barrier_semaphore()

    def greet(k, carry):
        pl.semaphore_signal(
            barrier, inc=1, device_id=(sec, (me + k) % MP), device_id_type=pl.DeviceIdType.MESH
        )
        return carry

    lax.fori_loop(1, MP, greet, 0)
    for s in (ypeer, dpeer, right, left, across):
        pl.semaphore_signal(
            barrier, inc=1, device_id=(s, me), device_id_type=pl.DeviceIdType.MESH
        )

    loads = [
        pltpu.make_async_copy(a, b, load_sem.at[i])
        for i, (a, b) in enumerate(
            (
                (x_hbm, x_v), (we_hbm, we_v), (wr_hbm, wr_v), (dec_hbm, dec_v), (wq_hbm, wq_v),
                (og_hbm, og_v), (mix_hbm, mix_v), (wk_hbm, wk_v), (wv_hbm, wv_v),
            )
        )
    ]
    for load in loads:
        load.start()

    loads[0].wait()
    normed = norm_rows(x_v[...], ig_ref[...]).astype(BF)
    values = x_v[...].astype(F32)
    for c in range(CHUNKS):
        wide[c] = values[:, c * 128 : (c + 1) * 128]
    for c in range(CHUNKS):
        for r in range(SHARE):
            res[pl.ds(r * CHUNKS + c, 1), :] = wide[c, pl.ds(SHARE * me + r, 1), :]
    loads[1].wait()
    hidden = jnp.maximum(dot(normed, we_v[...]), 0.0).astype(BF)
    loads[2].wait()
    part = dot(hidden, wr_v[...])
    for c in range(CHUNKS):
        wide[c] = part[:, c * 128 : (c + 1) * 128]
    for c in range(CHUNKS):
        for r in range(SHARE):
            stage[pl.ds(r * CHUNKS + c, MP, stride=PIECE), :] = wide[c, pl.ds(r, MP, stride=SHARE), :]
    send[...] = stage[...].reshape(MP, PIECE, 128).astype(BF)

    pl.semaphore_wait(barrier, MP - 1 + 5)

    def scatter(src, dst, ss, rs):
        def one(m):
            remote(src.at[m], dst.at[me], ss, rs, sec, m).start()

        one((me + MP // 2) % MP)

        def both(k, carry):
            d = MP // 2 - 1 - k
            one((me + d) % MP)
            one((me + MP - d) % MP)
            return carry

        lax.fori_loop(0, MP // 2 - 1, both, 0)
        dst[me] = src[me]

    def drained(src, dst, ss, rs):
        return remote(src.at[pl.ds(0, MP - 1)], dst.at[pl.ds(0, MP - 1)], ss, rs, sec, (me + 1) % MP)

    def summed(pieces):
        return jnp.sum(pieces[...].astype(F32), axis=0)

    scatter(send, recv, rs_s, rs_r)

    loads[3].wait()
    dec = norm_rows(dec_v[...], qg_ref[...]).astype(BF)
    loads[4].wait()
    tokens = pl.ds(pl.multiple_of(sec * QROWS, QROWS), QROWS)
    qg[tokens, 0:WIDTH] = dot(dec, wq_v[...]).astype(BF)
    loads[5].wait()
    loads[6].wait()
    qg[tokens, WIDTH : 2 * WIDTH] = dot_t(og_v[...], mix_v[...]).astype(BF)

    def rows_of(s, half=None):
        if half is None:
            return qg.at[pl.ds(pl.multiple_of(s * QROWS, QROWS), QROWS), :]
        return qg.at[pl.ds(pl.multiple_of(s * QROWS + half * (QROWS // 2), QROWS // 2), QROWS // 2), :]

    copies = []

    def forward(s, half, ss, rs, to):
        ref = rows_of(s, half)
        copy = remote(ref, ref, ss, rs, to, me)
        copy.start()
        copies.append(copy)

    def arrival(s, half, ss, rs):
        ref = rows_of(s, half)
        remote(ref, ref, ss, rs, dpeer, me).wait_recv()

    s_me, s_y = sec, ypeer
    s_r, s_l, s_a = right, left, across
    s_ry, s_ly, s_ay = section_of(1, 1, 0), section_of(3, 1, 0), section_of(2, 1, 0)
    forward(s_me, None, y_s, y_r, ypeer)
    forward(s_me, None, x_s.at[0], x_r.at[0], right)
    forward(s_me, None, x_s.at[1], x_r.at[1], left)
    forward(s_me, None, d_s.at[0], d_r.at[0], dpeer)
    arrival(s_l, None, x_s.at[0], x_r.at[0])
    forward(s_l, 0, h_s.at[0], h_r.at[0], right)
    forward(s_l, None, d_s.at[1], d_r.at[1], dpeer)
    arrival(s_r, None, x_s.at[1], x_r.at[1])
    forward(s_r, 1, h_s.at[1], h_r.at[1], left)
    forward(s_r, None, d_s.at[2], d_r.at[2], dpeer)

    rs_copy = drained(send, recv, rs_s, rs_r)
    rs_copy.wait_recv()
    rows = (summed(recv) + res[...]).reshape(SHARE, CHUNKS, 128)
    mean = jnp.sum(jnp.sum(rows * rows, axis=2, keepdims=True), axis=1, keepdims=True) * (1.0 / D)
    rows = rows * lax.rsqrt(mean + 1e-06) * fg_ref[...].reshape(1, CHUNKS, 128)
    own[...] = rows.reshape(PIECE, 128)
    gath[me] = own[...].astype(BF)

    def spread(m):
        remote(gath.at[me], gath.at[me], ag_s, ag_r, sec, m).start()

    spread((me + MP // 2) % MP)

    def both(k, carry):
        d = MP // 2 - 1 - k
        spread((me + d) % MP)
        spread((me + MP - d) % MP)
        return carry

    lax.fori_loop(0, MP // 2 - 1, both, 0)
    for r in range(SHARE):
        for c in range(CHUNKS):
            mem_out[r : r + 1, c * 128 : (c + 1) * 128] = own[
                r * CHUNKS + c : r * CHUNKS + c + 1, :
            ].astype(BF)

    arrival(s_y, None, y_s, y_r)
    forward(s_y, None, x_s.at[2], x_r.at[2], right)
    forward(s_y, None, x_s.at[3], x_r.at[3], left)
    forward(s_y, None, d_s.at[3], d_r.at[3], dpeer)
    arrival(s_a, 0, h_s.at[0], h_r.at[0])
    arrival(s_a, 1, h_s.at[1], h_r.at[1])
    forward(s_a, None, d_s.at[4], d_r.at[4], dpeer)
    arrival(s_ly, None, x_s.at[2], x_r.at[2])
    forward(s_ly, 0, h_s.at[2], h_r.at[2], right)
    forward(s_ly, None, d_s.at[5], d_r.at[5], dpeer)
    arrival(s_ry, None, x_s.at[3], x_r.at[3])
    forward(s_ry, 1, h_s.at[3], h_r.at[3], left)
    forward(s_ry, None, d_s.at[6], d_r.at[6], dpeer)

    ag_copy = drained(gath, gath, ag_s, ag_r)
    ag_copy.wait_recv()
    stage[...] = gath[...].reshape(MP * PIECE, 128).astype(F32)
    for r in range(SHARE):
        for c in range(CHUNKS):
            mem[r * MP : (r + 1) * MP, c * 128 : (c + 1) * 128] = stage[
                pl.ds(r * CHUNKS + c, MP, stride=PIECE), :
            ].astype(BF)
    loads[7].wait()
    keys = dot(mem[...], wk_v[...]).astype(BF)
    loads[8].wait()
    vals = dot(mem[...], wv_v[...]).astype(BF)

    arrival(s_ay, 0, h_s.at[2], h_r.at[2])
    arrival(s_ay, 1, h_s.at[3], h_r.at[3])
    forward(s_ay, None, d_s.at[7], d_r.at[7], dpeer)
    order = (
        section_of(0, 0, 1), section_of(3, 0, 1), section_of(1, 0, 1), section_of(0, 1, 1),
        section_of(2, 0, 1), section_of(3, 1, 1), section_of(1, 1, 1), section_of(2, 1, 1),
    )
    for i, s in enumerate(order):
        arrival(s, None, d_s.at[i], d_r.at[i])

    for h in range(2):
        key_h = keys[:, h * DK : (h + 1) * DK]
        val_h = vals[:, h * DK : (h + 1) * DK]

        def block(b, carry, h=h, key_h=key_h, val_h=val_h):
            at = pl.ds(pl.multiple_of(b * BLOCK, BLOCK), BLOCK)
            s = dot_t(key_h, qg[at, h * DK : (h + 1) * DK]) * SCALE
            pg = dot_t(val_h, qg[at, WIDTH + h * DK : WIDTH + (h + 1) * DK])
            top = jnp.max(s, axis=0, keepdims=True)
            w = jnp.exp(s - top)
            wts[h, b] = w
            pgr[h, b] = pg
            row = pl.ds(b, 1)
            stats[h, 0, row, :] = top
            stats[h, 1, row, :] = jnp.sum(w, axis=0, keepdims=True)
            stats[h, 2, row, :] = jnp.sum(w * pg, axis=0, keepdims=True)
            return carry

        lax.fori_loop(0, BLOCKS, block, 0)

    def three(ref):
        return ref[0], ref[1], ref[2]

    def put(ref, values):
        for i in range(3):
            ref[i] = values[i]

    sd = remote(stats.at[1 - core], got_d, sd_s, sd_r, dpeer, me)
    sd.start()
    sd.wait_recv()
    put(mid, merge(three(stats.at[core]), three(got_d)))
    sy = remote(mid, got_y, sy_s, sy_r, ypeer, me)
    sy.start()
    sy.wait_recv()
    put(pair, merge(three(mid), three(got_y)))
    sx = [
        remote(pair, got_x.at[i], sx_s.at[i], sx_r.at[i], to, me)
        for i, to in enumerate((across, right, left))
    ]
    for copy in sx:
        copy.start()
    sx[1].wait_recv()
    total = merge(three(pair), three(got_x.at[1]))
    sx[2].wait_recv()
    total = merge(total, three(got_x.at[2]))
    sx[0].wait_recv()
    put(fin.at[core], merge(total, three(got_x.at[0])))
    sf = remote(fin.at[core], fin.at[core], sf_s, sf_r, dpeer, me)
    sf.start()
    sf.wait_recv()

    sums = []
    for h in range(2):

        def block(b, carry, h=h):
            at = pl.ds(pl.multiple_of(b * BLOCK, BLOCK), BLOCK)
            row = pl.ds(b, 1)
            total = fin[h, 1, row, :]
            factor = jnp.exp(stats[h, 0, row, :] - fin[h, 0, row, :]) / total
            delta = fin[h, 2, row, :] / total
            probs = wts[h, b] * factor
            sg = (probs * (pgr[h, b] - delta) * SCALE).astype(BF)
            kg = carry[0] + dot(sg, qg[at, h * DK : (h + 1) * DK])
            vg = carry[1] + dot(probs.astype(BF), qg[at, WIDTH + h * DK : WIDTH + (h + 1) * DK])
            return kg, vg

        zero = jnp.zeros((ROWS, DK), F32)
        sums.append(lax.fori_loop(0, BLOCKS, block, (zero, zero)))
    kg = jnp.concatenate([s[0] for s in sums], axis=1).astype(BF)
    vg = jnp.concatenate([s[1] for s in sums], axis=1).astype(BF)
    part = dot_t(kg, wk_v[...]) + dot_t(vg, wv_v[...])
    for r in range(SHARE):
        for c in range(CHUNKS):
            stage[pl.ds(r * CHUNKS + c, MP, stride=PIECE), :] = part[
                r * MP : (r + 1) * MP, c * 128 : (c + 1) * 128
            ]
    send2[...] = stage[...].reshape(MP, PIECE, 128).astype(BF)
    scatter(send2, recv2, rs2_s, rs2_r)
    rs2_copy = drained(send2, recv2, rs2_s, rs2_r)

    rs_copy.wait_send()
    ag_copy.wait_send()
    for copy in copies + [sd, sy, sf] + sx:
        copy.wait_send()
    rs2_copy.wait_recv()
    own[...] = summed(recv2)
    for r in range(SHARE):
        for c in range(CHUNKS):
            grad_out[r : r + 1, c * 128 : (c + 1) * 128] = own[
                r * CHUNKS + c : r * CHUNKS + c + 1, :
            ].astype(BF)
    rs2_copy.wait_send()


def body(
    encoder_input, input_gain, expand_weight, reduce_weight, final_gain, decoder_input, query_gain,
    query_weight, key_weight, value_weight, mixing_weight, output_gradient,
):
    vmem = pl.BlockSpec(memory_space=pltpu.VMEM)
    hbm = pl.BlockSpec(memory_space=pl.ANY)
    dma = pltpu.SemaphoreType.DMA
    piece3 = (3, BLOCKS, BLOCK)
    out = jax.ShapeDtypeStruct((SHARE, D), BF)
    return pl.pallas_call(
        kernel,
        out_shape=(out, out),
        in_specs=[hbm, vmem, hbm, hbm, vmem, hbm, vmem, hbm, hbm, hbm, hbm, hbm],
        out_specs=(vmem, vmem),
        scratch_shapes=[
            pltpu.VMEM(encoder_input.shape, BF),
            pltpu.VMEM(expand_weight.shape, BF),
            pltpu.VMEM(reduce_weight.shape, BF),
            pltpu.VMEM(decoder_input.shape, BF),
            pltpu.VMEM(query_weight.shape, BF),
            pltpu.VMEM(key_weight.shape, BF),
            pltpu.VMEM(value_weight.shape, BF),
            pltpu.VMEM(mixing_weight.shape, BF),
            pltpu.VMEM(output_gradient.shape, BF),
            dma((9,)),
            pltpu.VMEM((CHUNKS, ROWS, 128), F32),
            pltpu.VMEM((MP * PIECE, 128), F32),
            pltpu.VMEM((PIECE, 128), F32),
            pltpu.VMEM((PIECE, 128), F32),
            pltpu.VMEM((MP, PIECE, 128), BF),
            pltpu.VMEM((MP, PIECE, 128), BF),
            pltpu.VMEM((MP, PIECE, 128), BF),
            pltpu.VMEM((MP, PIECE, 128), BF),
            pltpu.VMEM((MP, PIECE, 128), BF),
            pltpu.VMEM((ROWS, D), BF),
            pltpu.VMEM((QALL, 2 * WIDTH), BF),
            pltpu.VMEM((2, BLOCKS, ROWS, BLOCK), F32),
            pltpu.VMEM((2, BLOCKS, ROWS, BLOCK), F32),
            pltpu.VMEM((2, *piece3), F32),
            pltpu.VMEM(piece3, F32),
            pltpu.VMEM(piece3, F32),
            pltpu.VMEM(piece3, F32),
            pltpu.VMEM(piece3, F32),
            pltpu.VMEM((3, *piece3), F32),
            pltpu.VMEM((2, *piece3), F32),
            dma, dma, dma, dma, dma, dma,
            dma, dma, dma((4,)), dma((4,)), dma((4,)), dma((4,)), dma((8,)), dma((8,)),
            dma, dma, dma, dma, dma((3,)), dma((3,)), dma, dma,
        ],
        compiler_params=pltpu.CompilerParams(
            collective_id=0, has_side_effects=True, vmem_limit_bytes=60 * 1024 * 1024
        ),
    )(
        encoder_input, input_gain.reshape(1, D), expand_weight, reduce_weight,
        final_gain.reshape(CHUNKS, 128), decoder_input, query_gain.reshape(1, D), query_weight,
        key_weight, value_weight, mixing_weight, output_gradient,
    )


def solution(mesh):
    in_specs = (
        P("section", None), P(), P(None, "mp"), P("mp", None), P(), P("section", None), P(),
        P(None, "mp"), P(None, "mp"), P(None, "mp"), P("mp", None), P("section", None),
    )
    out_specs = (P(("section", "mp"), None), P(("section", "mp"), None))
    return jax.shard_map(body, mesh=mesh, in_specs=in_specs, out_specs=out_specs, check_vma=False)
```

time: 241 us -> 97 us (0.40)
  blocking collectives: 122 us -> 0 us
  Pallas kernels: 0 us -> 93.5 us
  waiting for transfers between devices: 57.8 us -> 0 us
  starting transfers between devices: 19.4 us -> 0 us
  between operations: 14.3 us -> 0.64 us
  matrix products: 12.5 us -> 0 us
  other arithmetic: 7.33 us -> 0 us
  local copies, waits for them, and re-layouts: 6.14 us -> 2.6 us
    all_to_all x3 -> x0, blocking collectives: 122 us -> none  [the longest x2 80.5 us: from_everyone(): lax.all_to_all(jnp.broadcast_to(x[None], (length, *x.shape)), axis, 0, 0,...]
    pallas_call x0 -> x1, Pallas kernels: none -> 93.5 us  [body(): pl.pallas_call(kernel, out_shape=(out, out), in_specs=[hbm, vmem, hbm, hb...]
    all_to_all x1 -> x0, waiting for transfers between devices: 31.7 us -> none  [sum_at_owner(): pieces = lax.all_to_all(cut_along(x, dim, length), axis, 0, 0, tiled=True)]
    all_gather x1 -> x0, waiting for transfers between devices: 26 us -> none  [in_one_piece(): lax.all_gather(both, axis, axis=dim, tiled=True)]
    all_to_all x1 -> x0, starting transfers between devices: 19.4 us -> none  [sum_at_owner(): pieces = lax.all_to_all(cut_along(x, dim, length), axis, 0, 0, tiled=True)]
    dot_general x11 -> x0, matrix products: 12.5 us -> none  [the longest x1 2.49 us: body(): jnp.dot(hidden, reduce_weight, preferred_element_type=jnp.float32)]
    reduce_sum x5 -> x0, other arithmetic: 4.24 us -> none  [the longest x3 3.36 us: norm_rows(): jnp.mean(values * values, axis=-1, keepdims=True) + 1e-06]
    slice x2 -> x0, local copies, waits for them, and re-layouts: 3.29 us -> none  [the longest x1 2.49 us: in_one_piece(): lax.slice_in_dim(filled, at, at + a.shape[along], axis=along)]
  transfers between devices with their start and end apart: 2 -> 0, of which waited for: 2 -> 0; matrix products, arithmetic and copies ran while one was open for 4% -> 0% of each run, Pallas kernels for 0% -> 0%
where the time goes in v1:
time: 97 us; the launch traced here: 96.7 us
  Pallas kernels  93.5 us (96%)
  local copies, waits for them, and re-layouts  2.6 us (3%)
    pallas_call x1, Pallas kernels, body(): pl.pallas_call(kernel, out_shape=(out, out), in_specs=[hbm, vmem, hbm, hb...  93.5 us
    unnamed x2, local copies, waits for them, and re-layouts  2.6 us

profile of v1, /device:TPU:1, one launch (start us, length us, event | category | flops | bytes accessed | tf_op | source)
XLA Modules:
  0.0 96.7 jit_solution(16954213207242553879)
XLA Ops:
  0.6 93.5 %shard_map.131 = (bf16[3,1024]{1,0:T(4,128)(2,1)}, bf16[3,1024]{1,0:T(4,128)(2,1)}) custom-call(bf16[144,1024]{1,0:T(8,128)(2,1)} %x_hbm.1, f32[1,1024]{1,0:T(1,128)} %bitcast.3, bf16[1024,1024]{1,0:T(8,128)(2,1)} %we_hbm.1, bf16[1024,1024]{1,0:T(8,128)(2,1)} %wr_hbm.1, f32[8,128]{1,0:T(8,128)} %bitcast.4, bf16[256,1024]{1,0:T(8,128)(2,1)} %dec_hbm.1, ...), custom_call_target="tpu_custom_call" | custom-call | tf_op jit(solution)/shard_map/pallas_call | solution.py:349
  94.1 1.3 %copy.16 = bf16[3,1024]{1,0:T(4,128)(2,1)} copy(bf16[3,1024]{1,0:T(4,128)(2,1)} %get-tuple-element.4) | data formatting | bytes 12288
  95.4 1.3 %copy.17 = bf16[3,1024]{1,0:T(4,128)(2,1)} copy(bf16[3,1024]{1,0:T(4,128)(2,1)} %get-tuple-element.5) | data formatting | bytes 12288

commit v2 on v1

v2 whole, which is shorter than its diff:
```python
import jax
import jax.numpy as jnp
from jax import lax
from jax.experimental import pallas as pl
from jax.experimental.pallas import tpu as pltpu
from jax.sharding import PartitionSpec as P

DK = 128
D = 1024
CHUNKS = D // 128
ZS, YS = 12, 4
MP = ZS * YS
ROWS = 144
SHARE = ROWS // MP
PIECE = SHARE * CHUNKS
HEAD, TAIL = CHUNKS, PIECE - CHUNKS
QROWS = 256
QALL = 4096
BLOCK = 512
BLOCKS = QALL // BLOCK
WIDTH = 2 * DK
SCALE = DK ** (-0.5)
BF = jnp.bfloat16
F32 = jnp.float32


def dot(a, b):
    return jnp.dot(a, b, preferred_element_type=F32)


def dot_t(a, b):
    return lax.dot_general(a, b, (((1,), (1,)), ((), ())), preferred_element_type=F32)


def norm_rows(rows, gain):
    values = rows.astype(F32)
    return values * lax.rsqrt(jnp.mean(values * values, axis=-1, keepdims=True) + 1e-06) * gain


def merge(a, b):
    top = jnp.maximum(a[0], b[0])
    left = jnp.exp(a[0] - top)
    right = jnp.exp(b[0] - top)
    return top, a[1] * left + b[1] * right, a[2] * left + b[2] * right


def kernel(
    x_hbm, ig_ref, we_hbm, wr_hbm, fg_ref, dec_hbm, qg_ref, wq_hbm, wk_hbm, wv_hbm, mix_hbm, og_hbm,
    mem_out, grad_out,
    x_v, we_v, wr_v, dec_v, wq_v, wk_v, wv_v, mix_v, og_v, load_sem,
    wide, stage, own, res, bufs1, bufs2, gath_a, gath_b, mem,
    qg, wts, pgr, stats, got_d, mid, got_y, pair, got_x, fin, grads,
    rs_sems, ag_sems, rs2_sems,
    y_s, y_r, x_s, x_r, d_s, d_r,
    sd_s, sd_r, sy_s, sy_r, sx_s, sx_r, sf_s, sf_r,
):
    sec = lax.axis_index("section")
    me = lax.axis_index("mp")
    xi = sec // 4
    yi = (sec // 2) % 2
    core = sec % 2
    zi, yl = me // YS, me % YS

    def section_of(dx, dy, dc):
        return (((xi + dx) % 4) * 2 + (yi + dy) % 2) * 2 + (core + dc) % 2

    ypeer, dpeer = section_of(0, 1, 0), section_of(0, 0, 1)
    right, left, across = section_of(1, 0, 0), section_of(3, 0, 0), section_of(2, 0, 0)

    def remote(src, dst, ss, rs, s, m):
        return pltpu.make_async_remote_copy(
            src_ref=src, dst_ref=dst, send_sem=ss, recv_sem=rs, device_id=(s, m),
            device_id_type=pl.DeviceIdType.MESH,
        )

    loads = [
        pltpu.make_async_copy(a, b, load_sem.at[i])
        for i, (a, b) in enumerate(
            (
                (x_hbm, x_v), (we_hbm, we_v), (wr_hbm, wr_v), (dec_hbm, dec_v), (wq_hbm, wq_v),
                (og_hbm, og_v), (mix_hbm, mix_v), (wk_hbm, wk_v), (wv_hbm, wv_v),
            )
        )
    ]
    for load in loads:
        load.start()

    barrier = pltpu.get_barrier_semaphore()

    def greet(s, m):
        pl.semaphore_signal(barrier, inc=1, device_id=(s, m), device_id_type=pl.DeviceIdType.MESH)

    z_peers = [((zi + k) % ZS, ((zi + k) % ZS) * YS + yl) for k in (6, 5, 7, 4, 8, 3, 9, 2, 10, 1, 11)]
    y_peers = [((yl + k) % YS, zi * YS + (yl + k) % YS) for k in (2, 1, 3)]

    for _, m in z_peers + y_peers:
        greet(sec, m)
    for s in (ypeer, across, right, left, dpeer):
        greet(s, me)

    def pack(bufs):
        pieces = stage[...].reshape(ZS, YS, PIECE, 128)
        head = bufs[0].shape[2]
        for k in range(YS):
            bufs[0][k] = pieces[:, k, :head].astype(BF)
        bufs[4][...] = pieces[:, :, head:].astype(BF)

    started = []

    def post(src, dst, sems, i, m):
        copy = remote(src, dst, sems.at[i], sems.at[i + 1], sec, m)
        copy.start()
        return copy

    def all_of(src, dst, sems, i, count):
        copy = remote(
            src.at[pl.ds(0, count)], dst.at[pl.ds(0, count)], sems.at[i], sems.at[i + 1], sec,
            y_peers[0][1],
        )
        started.append(copy)
        return copy

    def spread(src, dst, own_index, peers, sems, i):
        for k, m in peers:
            post(src.at[k], dst.at[own_index], sems, i, m)
        dst[own_index] = src[own_index]

    def added(pieces):
        return jnp.sum(pieces[...].astype(F32), axis=0)

    def reduce_first(bufs, sems):
        spread(bufs[0], bufs[1], yl, y_peers, sems, 0)
        spread(bufs[4], bufs[5], zi, z_peers, sems, 4)

    def reduce_turn(bufs, sems):
        all_of(bufs[0], bufs[1], sems, 0, YS - 1).wait_recv()
        bufs[2][...] = added(bufs[1]).astype(BF)
        spread(bufs[2], bufs[3], zi, z_peers, sems, 2)
        all_of(bufs[4], bufs[5], sems, 4, ZS - 1).wait_recv()
        bufs[6][...] = added(bufs[5]).astype(BF)
        spread(bufs[6], bufs[7], yl, y_peers, sems, 6)

    def reduce_last(bufs, sems):
        all_of(bufs[2], bufs[3], sems, 2, ZS - 1).wait_recv()
        own[: bufs[3].shape[1]] = added(bufs[3])
        all_of(bufs[6], bufs[7], sems, 6, YS - 1).wait_recv()
        own[bufs[3].shape[1] :] = added(bufs[7])

    loads[0].wait()
    normed = norm_rows(x_v[...], ig_ref[...]).astype(BF)
    values = x_v[...].astype(F32)
    for c in range(CHUNKS):
        wide[c] = values[:, c * 128 : (c + 1) * 128]
    for c in range(CHUNKS):
        for r in range(SHARE):
            res[pl.ds(r * CHUNKS + c, 1), :] = wide[c, pl.ds(SHARE * me + r, 1), :]
    loads[1].wait()
    hidden = jnp.maximum(dot(normed, we_v[...]), 0.0).astype(BF)
    loads[2].wait()
    part = dot(hidden, wr_v[...])
    for c in range(CHUNKS):
        wide[c] = part[:, c * 128 : (c + 1) * 128]
    for c in range(CHUNKS):
        for r in range(SHARE):
            stage[pl.ds(r * CHUNKS + c, MP, stride=PIECE), :] = wide[c, pl.ds(r, MP, stride=SHARE), :]
    pack(bufs1)

    loads[3].wait()
    dec = norm_rows(dec_v[...], qg_ref[...]).astype(BF)
    loads[4].wait()
    tokens = pl.ds(pl.multiple_of(sec * QROWS, QROWS), QROWS)
    qg[tokens, 0:WIDTH] = dot(dec, wq_v[...]).astype(BF)
    loads[5].wait()
    loads[6].wait()
    qg[tokens, WIDTH : 2 * WIDTH] = dot_t(og_v[...], mix_v[...]).astype(BF)

    pl.semaphore_wait(barrier, len(z_peers) + len(y_peers) + 5)

    def rows_of(s, half=None):
        if half is None:
            return qg.at[pl.ds(pl.multiple_of(s * QROWS, QROWS), QROWS), :]
        return qg.at[pl.ds(pl.multiple_of(s * QROWS + half * (QROWS // 2), QROWS // 2), QROWS // 2), :]

    copies = []

    def forward(s, half, sems, i, to):
        ref = rows_of(s, half)
        copy = remote(ref, ref, sems[0].at[i], sems[1].at[i], to, me)
        copy.start()
        copies.append(copy)

    def arrival(s, half, sems, i):
        ref = rows_of(s, half)
        remote(ref, ref, sems[0].at[i], sems[1].at[i], dpeer, me).wait_recv()

    ys, xs, ds = (y_s, y_r), (x_s, x_r), (d_s, d_r)

    def along_x(s, half, i):
        for k, to in enumerate((right, left, across)):
            forward(s, half, xs, 3 * i + k, to)

    reduce_first(bufs1, rs_sems)
    forward(sec, 0, ys, 0, ypeer)
    along_x(sec, None, 0)
    forward(sec, None, ds, 0, dpeer)

    reduce_turn(bufs1, rs_sems)
    forward(sec, 1, ys, 1, ypeer)
    reduce_last(bufs1, rs_sems)
    rows = (own[...] + res[...]).reshape(SHARE, CHUNKS, 128)
    mean = jnp.sum(jnp.sum(rows * rows, axis=2, keepdims=True), axis=1, keepdims=True) * (1.0 / D)
    rows = rows * lax.rsqrt(mean + 1e-06) * fg_ref[...].reshape(1, CHUNKS, 128)
    own[...] = rows.reshape(PIECE, 128)
    gath_a[yl, zi] = own[:HEAD].astype(BF)
    gath_b[zi, yl] = own[HEAD:].astype(BF)
    for _, m in y_peers:
        post(gath_b.at[zi, yl], gath_b.at[zi, yl], ag_sems, 4, m)
    for _, m in z_peers:
        post(gath_a.at[yl, zi], gath_a.at[yl, zi], ag_sems, 0, m)
    for r in range(SHARE):
        for c in range(CHUNKS):
            mem_out[r : r + 1, c * 128 : (c + 1) * 128] = own[
                r * CHUNKS + c : r * CHUNKS + c + 1, :
            ].astype(BF)

    arrival(ypeer, 0, ys, 0)
    along_x(ypeer, 0, 1)
    forward(ypeer, 0, ds, 4, dpeer)
    all_of(gath_b.at[zi], gath_b.at[zi], ag_sems, 4, YS - 1).wait_recv()
    for _, m in z_peers:
        post(gath_b.at[zi], gath_b.at[zi], ag_sems, 6, m)
    near = ((section_of(3, 0, 0), 0), (section_of(1, 0, 0), 1), (section_of(2, 0, 0), 2))
    far = ((section_of(3, 1, 0), 0), (section_of(1, 1, 0), 1), (section_of(2, 1, 0), 2))
    all_of(gath_a.at[yl], gath_a.at[yl], ag_sems, 0, ZS - 1).wait_recv()
    for _, m in y_peers:
        post(gath_a.at[yl], gath_a.at[yl], ag_sems, 2, m)
    for s, k in near:
        arrival(s, None, xs, k)
        forward(s, None, ds, 1 + k, dpeer)
    arrival(ypeer, 1, ys, 1)
    along_x(ypeer, 1, 2)
    forward(ypeer, 1, ds, 5, dpeer)

    all_of(gath_b, gath_b, ag_sems, 6, ZS - 1).wait_recv()
    all_of(gath_a, gath_a, ag_sems, 2, YS - 1).wait_recv()
    for z in range(ZS):
        for y in range(YS):
            at = (z * YS + y) * PIECE
            stage[at : at + HEAD] = gath_a[y, z].astype(F32)
            stage[at + HEAD : at + PIECE] = gath_b[z, y].astype(F32)
    for r in range(SHARE):
        for c in range(CHUNKS):
            mem[r * MP : (r + 1) * MP, c * 128 : (c + 1) * 128] = stage[
                pl.ds(r * CHUNKS + c, MP, stride=PIECE), :
            ].astype(BF)
    loads[7].wait()
    keys = dot(mem[...], wk_v[...]).astype(BF)
    loads[8].wait()
    vals = dot(mem[...], wv_v[...]).astype(BF)

    def block(b):
        at = pl.ds(pl.multiple_of(b * BLOCK, BLOCK), BLOCK)
        row = pl.ds(b, 1)
        for h in range(2):
            s = dot_t(keys[:, h * DK : (h + 1) * DK], qg[at, h * DK : (h + 1) * DK]) * SCALE
            pg = dot_t(
                vals[:, h * DK : (h + 1) * DK], qg[at, WIDTH + h * DK : WIDTH + (h + 1) * DK]
            )
            top = jnp.max(s, axis=0, keepdims=True)
            w = jnp.exp(s - top)
            wts[h, b] = w
            pgr[h, b] = pg
            stats[h, 0, row, :] = top
            stats[h, 1, row, :] = jnp.sum(w, axis=0, keepdims=True)
            stats[h, 2, row, :] = jnp.sum(w * pg, axis=0, keepdims=True)

    arrival(section_of(0, 0, 1), None, ds, 0)
    block(sec // 2)
    for k, dx in enumerate((3, 1, 2)):
        arrival(section_of(dx, 0, 1), None, ds, 1 + k)
        block(section_of(dx, 0, 0) // 2)
    for half in range(2):
        for s, k in far:
            arrival(s, half, xs, 3 * (half + 1) + k)
            forward(s, half, ds, 6 + 3 * half + k, dpeer)
    for half in range(2):
        arrival(section_of(0, 1, 1), half, ds, 4 + half)
    block(ypeer // 2)
    for k, dx in enumerate((3, 1, 2)):
        for half in range(2):
            arrival(section_of(dx, 1, 1), half, ds, 6 + 3 * half + k)
        block(section_of(dx, 1, 0) // 2)

    def three(ref):
        return ref[0], ref[1], ref[2]

    def put(ref, values):
        for i in range(3):
            ref[i] = values[i]

    sd = remote(stats.at[1 - core], got_d, sd_s, sd_r, dpeer, me)
    sd.start()
    sd.wait_recv()
    put(mid, merge(three(stats.at[core]), three(got_d)))
    sy = remote(mid, got_y, sy_s, sy_r, ypeer, me)
    sy.start()
    sy.wait_recv()
    put(pair, merge(three(mid), three(got_y)))
    sx = [
        remote(pair, got_x.at[i], sx_s.at[i], sx_r.at[i], to, me)
        for i, to in enumerate((across, right, left))
    ]
    for copy in sx:
        copy.start()
    sx[1].wait_recv()
    total = merge(three(pair), three(got_x.at[1]))
    sx[2].wait_recv()
    total = merge(total, three(got_x.at[2]))
    sx[0].wait_recv()
    put(fin.at[core], merge(total, three(got_x.at[0])))
    sf = remote(fin.at[core], fin.at[core], sf_s, sf_r, dpeer, me)
    sf.start()

    def gradients(h):
        lanes = pl.ds(pl.multiple_of(h * DK, DK), DK)
        grad_lanes = pl.ds(pl.multiple_of(WIDTH + h * DK, DK), DK)

        def one(b, carry):
            at = pl.ds(pl.multiple_of(b * BLOCK, BLOCK), BLOCK)
            row = pl.ds(b, 1)
            total = fin[h, 1, row, :]
            factor = jnp.exp(stats[h, 0, row, :] - fin[h, 0, row, :]) / total
            delta = fin[h, 2, row, :] / total
            probs = wts[h, b] * factor
            sg = (probs * (pgr[h, b] - delta) * SCALE).astype(BF)
            kg = carry[0] + dot(sg, qg[at, lanes])
            vg = carry[1] + dot(probs.astype(BF), qg[at, grad_lanes])
            return kg, vg

        zero = jnp.zeros((ROWS, DK), F32)
        kg, vg = lax.fori_loop(0, BLOCKS, one, (zero, zero), unroll=2)
        grads[0, :, lanes] = kg.astype(BF)
        grads[1, :, lanes] = vg.astype(BF)

    gradients(core)
    sf.wait_recv()
    gradients(1 - core)
    part = dot_t(grads[0], wk_v[...]) + dot_t(grads[1], wv_v[...])
    for r in range(SHARE):
        for c in range(CHUNKS):
            stage[pl.ds(r * CHUNKS + c, MP, stride=PIECE), :] = part[
                r * MP : (r + 1) * MP, c * 128 : (c + 1) * 128
            ]
    pack(bufs2)
    reduce_first(bufs2, rs2_sems)
    reduce_turn(bufs2, rs2_sems)
    reduce_last(bufs2, rs2_sems)

    for copy in started + copies + [sd, sy, sf] + sx:
        copy.wait_send()
    for r in range(SHARE):
        for c in range(CHUNKS):
            grad_out[r : r + 1, c * 128 : (c + 1) * 128] = own[
                r * CHUNKS + c : r * CHUNKS + c + 1, :
            ].astype(BF)


def body(
    encoder_input, input_gain, expand_weight, reduce_weight, final_gain, decoder_input, query_gain,
    query_weight, key_weight, value_weight, mixing_weight, output_gradient,
):
    vmem = pl.BlockSpec(memory_space=pltpu.VMEM)
    hbm = pl.BlockSpec(memory_space=pl.ANY)
    dma = pltpu.SemaphoreType.DMA
    piece3 = (3, BLOCKS, BLOCK)

    def sums_at_owner(head):
        tail = PIECE - head
        shapes = (
            (YS, ZS, head, 128), (YS, ZS, head, 128), (ZS, head, 128), (ZS, head, 128),
            (ZS, YS, tail, 128), (ZS, YS, tail, 128), (YS, tail, 128), (YS, tail, 128),
        )
        return [pltpu.VMEM(shape, BF) for shape in shapes]

    out = jax.ShapeDtypeStruct((SHARE, D), BF)
    return pl.pallas_call(
        kernel,
        out_shape=(out, out),
        in_specs=[hbm, vmem, hbm, hbm, vmem, hbm, vmem, hbm, hbm, hbm, hbm, hbm],
        out_specs=(vmem, vmem),
        scratch_shapes=[
            pltpu.VMEM(encoder_input.shape, BF),
            pltpu.VMEM(expand_weight.shape, BF),
            pltpu.VMEM(reduce_weight.shape, BF),
            pltpu.VMEM(decoder_input.shape, BF),
            pltpu.VMEM(query_weight.shape, BF),
            pltpu.VMEM(key_weight.shape, BF),
            pltpu.VMEM(value_weight.shape, BF),
            pltpu.VMEM(mixing_weight.shape, BF),
            pltpu.VMEM(output_gradient.shape, BF),
            dma((9,)),
            pltpu.VMEM((CHUNKS, ROWS, 128), F32),
            pltpu.VMEM((MP * PIECE, 128), F32),
            pltpu.VMEM((PIECE, 128), F32),
            pltpu.VMEM((PIECE, 128), F32),
            sums_at_owner(1 * CHUNKS),
            sums_at_owner(2 * CHUNKS),
            pltpu.VMEM((YS, ZS, HEAD, 128), BF),
            pltpu.VMEM((ZS, YS, TAIL, 128), BF),
            pltpu.VMEM((ROWS, D), BF),
            pltpu.VMEM((QALL, 2 * WIDTH), BF),
            pltpu.VMEM((2, BLOCKS, ROWS, BLOCK), F32),
            pltpu.VMEM((2, BLOCKS, ROWS, BLOCK), F32),
            pltpu.VMEM((2, *piece3), F32),
            pltpu.VMEM(piece3, F32),
            pltpu.VMEM(piece3, F32),
            pltpu.VMEM(piece3, F32),
            pltpu.VMEM(piece3, F32),
            pltpu.VMEM((3, *piece3), F32),
            pltpu.VMEM((2, *piece3), F32),
            pltpu.VMEM((2, ROWS, WIDTH), BF),
            dma((8,)), dma((8,)), dma((8,)),
            dma((2,)), dma((2,)), dma((9,)), dma((9,)), dma((12,)), dma((12,)),
            dma, dma, dma, dma, dma((3,)), dma((3,)), dma, dma,
        ],
        compiler_params=pltpu.CompilerParams(
            collective_id=0, has_side_effects=True, vmem_limit_bytes=60 * 1024 * 1024
        ),
    )(
        encoder_input, input_gain.reshape(1, D), expand_weight, reduce_weight,
        final_gain.reshape(CHUNKS, 128), decoder_input, query_gain.reshape(1, D), query_weight,
        key_weight, value_weight, mixing_weight, output_gradient,
    )


def solution(mesh):
    in_specs = (
        P("section", None), P(), P(None, "mp"), P("mp", None), P(), P("section", None), P(),
        P(None, "mp"), P(None, "mp"), P(None, "mp"), P("mp", None), P("section", None),
    )
    out_specs = (P(("section", "mp"), None), P(("section", "mp"), None))
    return jax.shard_map(body, mesh=mesh, in_specs=in_specs, out_specs=out_specs, check_vma=False)
```

time: 97 us -> 81.3 us (0.84)
  Pallas kernels: 93.5 us -> 77.6 us
    pallas_call x1, Pallas kernels: 93.5 us -> 77.6 us  [body(): pl.pallas_call(kernel, out_shape=(out, out), in_specs=[hbm, vmem, hbm, hb...]
where the time goes in v2:
time: 81.3 us; the launch traced here: 80.8 us
  Pallas kernels  77.6 us (95%)
  local copies, waits for them, and re-layouts  2.6 us (3%)
    pallas_call x1, Pallas kernels, body(): pl.pallas_call(kernel, out_shape=(out, out), in_specs=[hbm, vmem, hbm, hb...  77.6 us
    unnamed x2, local copies, waits for them, and re-layouts  2.6 us

profile of v2, /device:TPU:1, one launch (start us, length us, event | category | flops | bytes accessed | tf_op | source)
XLA Modules:
  0.0 80.8 jit_solution(9341437675198150562)
XLA Ops:
  0.6 77.6 %shard_map.131 = (bf16[3,1024]{1,0:T(4,128)(2,1)}, bf16[3,1024]{1,0:T(4,128)(2,1)}) custom-call(bf16[144,1024]{1,0:T(8,128)(2,1)} %x_hbm.1, f32[1,1024]{1,0:T(1,128)} %bitcast.3, bf16[1024,1024]{1,0:T(8,128)(2,1)} %we_hbm.1, bf16[1024,1024]{1,0:T(8,128)(2,1)} %wr_hbm.1, f32[8,128]{1,0:T(8,128)} %bitcast.4, bf16[256,1024]{1,0:T(8,128)(2,1)} %dec_hbm.1, ...), custom_call_target="tpu_custom_call" | custom-call | tf_op jit(solution)/shard_map/pallas_call | solution.py:386
  78.2 1.3 %copy.16 = bf16[3,1024]{1,0:T(4,128)(2,1)} copy(bf16[3,1024]{1,0:T(4,128)(2,1)} %get-tuple-element.4) | data formatting | bytes 12288
  79.5 1.3 %copy.17 = bf16[3,1024]{1,0:T(4,128)(2,1)} copy(bf16[3,1024]{1,0:T(4,128)(2,1)} %get-tuple-element.5) | data formatting | bytes 12288

commit v3 on v2

v3 whole, which is shorter than its diff:
```python
import jax
import jax.numpy as jnp
from jax import lax
from jax.experimental import pallas as pl
from jax.experimental.pallas import tpu as pltpu
from jax.sharding import PartitionSpec as P

DK = 128
D = 1024
CHUNKS = D // 128
ZS, YS = 12, 4
MP = ZS * YS
ROWS = 144
SHARE = ROWS // MP
PIECE = SHARE * CHUNKS
HEAD, TAIL = 2 * CHUNKS, PIECE - 2 * CHUNKS
QROWS = 256
QALL = 4096
BLOCK = 512
BLOCKS = QALL // BLOCK
WIDTH = 2 * DK
SCALE = DK ** (-0.5)
LOG2E = 1.4426950408889634
TILE = 256
BF = jnp.bfloat16
F32 = jnp.float32


def dot(a, b):
    return jnp.dot(a, b, preferred_element_type=F32)


def dot_t(a, b):
    return lax.dot_general(a, b, (((1,), (1,)), ((), ())), preferred_element_type=F32)


def norm_rows(rows, gain):
    values = rows.astype(F32)
    return values * lax.rsqrt(jnp.mean(values * values, axis=-1, keepdims=True) + 1e-06) * gain


def merge(a, b):
    top = jnp.maximum(a[0], b[0])
    left = jnp.exp2(a[0] - top)
    right = jnp.exp2(b[0] - top)
    total = left + right
    return top + jnp.log(total) * LOG2E, (a[1] * left + b[1] * right) / total


def kernel(
    x_hbm, ig_ref, we_hbm, wr_hbm, fg_ref, dec_hbm, qg_ref, wq_hbm, wk_hbm, wv_hbm, mix_hbm, og_hbm,
    outs,
    x_v, we_v, wr_v, dec_v, wq_v, wk_v, wv_v, mix_v, og_v, load_sem,
    wide, stage, own, res, bufs1, bufs2, gath_a, gath_b, mem,
    qg, wts, pgr, tops, stats, got_d, mid, got_y, pair, got_x, fin, grads,
    rs_sems, ag_sems, rs2_sems,
    qg_s, y_r, x_r, d_r, st_s, sx_s, sd_r, sy_r, sx_r, sf_r,
):
    sec = lax.axis_index("section")
    me = lax.axis_index("mp")
    xi = sec // 4
    yi = (sec // 2) % 2
    core = sec % 2
    zi, yl = me // YS, me % YS

    def section_of(dx, dy, dc):
        return (((xi + dx) % 4) * 2 + (yi + dy) % 2) * 2 + (core + dc) % 2

    ypeer, dpeer = section_of(0, 1, 0), section_of(0, 0, 1)
    right, left, across = section_of(1, 0, 0), section_of(3, 0, 0), section_of(2, 0, 0)

    def remote(src, dst, ss, rs, s, m):
        return pltpu.make_async_remote_copy(
            src_ref=src, dst_ref=dst, send_sem=ss, recv_sem=rs, device_id=(s, m),
            device_id_type=pl.DeviceIdType.MESH,
        )

    def load(a, b, i):
        copy = pltpu.make_async_copy(a, b, load_sem.at[i])
        copy.start()
        return copy

    def load_quarters(a, b, i):
        rows = a.shape[0] // 4
        for k in range(4):
            load(a.at[pl.ds(k * rows, rows)], b.at[pl.ds(k * rows, rows)], i)
        return pltpu.make_async_copy(a, b, load_sem.at[i])

    x_load = load(x_hbm, x_v, 0)
    we_load = load_quarters(we_hbm, we_v, 1)
    wr_load = load_quarters(wr_hbm, wr_v, 2)

    barrier = pltpu.get_barrier_semaphore()

    def greet(s, m):
        pl.semaphore_signal(barrier, inc=1, device_id=(s, m), device_id_type=pl.DeviceIdType.MESH)

    z_peers = [((zi + k) % ZS, ((zi + k) % ZS) * YS + yl) for k in (6, 5, 7, 4, 8, 3, 9, 2, 10, 1, 11)]
    y_peers = [((yl + k) % YS, zi * YS + (yl + k) % YS) for k in (2, 1, 3)]

    for _, m in z_peers + y_peers:
        greet(sec, m)
    for s in (ypeer, across, right, left, dpeer):
        greet(s, me)

    def pack_y(bufs):
        pieces = stage[...].reshape(ZS, YS, PIECE, 128)
        for k in range(YS):
            bufs[0][k] = pieces[:, k, : bufs[0].shape[2]].astype(BF)

    def pack_z(bufs):
        pieces = stage[...].reshape(ZS, YS, PIECE, 128)
        bufs[4][...] = pieces[:, :, bufs[0].shape[2] :].astype(BF)

    started = []

    def post(src, dst, sems, i, m):
        copy = remote(src, dst, sems.at[i], sems.at[i + 1], sec, m)
        copy.start()
        return copy

    def all_of(src, dst, sems, i, count):
        copy = remote(
            src.at[pl.ds(0, count)], dst.at[pl.ds(0, count)], sems.at[i], sems.at[i + 1], sec,
            y_peers[0][1],
        )
        started.append(copy)
        return copy

    def spread(src, dst, own_index, peers, sems, i):
        for k, m in peers:
            post(src.at[k], dst.at[own_index], sems, i, m)
        dst[own_index] = src[own_index]

    def added(pieces):
        return jnp.sum(pieces[...].astype(F32), axis=0)

    def reduce_turn(bufs, sems):
        all_of(bufs[0], bufs[1], sems, 0, YS - 1).wait_recv()
        bufs[2][...] = added(bufs[1]).astype(BF)
        spread(bufs[2], bufs[3], zi, z_peers, sems, 2)
        all_of(bufs[4], bufs[5], sems, 4, ZS - 1).wait_recv()
        bufs[6][...] = added(bufs[5]).astype(BF)
        spread(bufs[6], bufs[7], yl, y_peers, sems, 6)

    def reduce_last(bufs, sems):
        all_of(bufs[2], bufs[3], sems, 2, ZS - 1).wait_recv()
        own[: bufs[3].shape[1]] = added(bufs[3])
        all_of(bufs[6], bufs[7], sems, 6, YS - 1).wait_recv()
        own[bufs[3].shape[1] :] = added(bufs[7])

    x_load.wait()
    normed = norm_rows(x_v[...], ig_ref[...]).astype(BF)
    values = x_v[...].astype(F32)
    for c in range(CHUNKS):
        wide[c] = values[:, c * 128 : (c + 1) * 128]
    for c in range(CHUNKS):
        for r in range(SHARE):
            res[pl.ds(r * CHUNKS + c, 1), :] = wide[c, pl.ds(SHARE * me + r, 1), :]
    we_load.wait()
    loads = [
        load(a, b, 3 + i)
        for i, (a, b) in enumerate(
            (
                (dec_hbm, dec_v), (wq_hbm, wq_v), (og_hbm, og_v), (mix_hbm, mix_v), (wk_hbm, wk_v),
                (wv_hbm, wv_v),
            )
        )
    ]
    hidden = jnp.maximum(dot(normed, we_v[...]), 0.0).astype(BF)
    wr_load.wait()
    part = dot(hidden, wr_v[...])
    for c in range(CHUNKS):
        wide[c] = part[:, c * 128 : (c + 1) * 128]
    for c in range(CHUNKS):
        for r in range(SHARE):
            stage[pl.ds(r * CHUNKS + c, MP, stride=PIECE), :] = wide[c, pl.ds(r, MP, stride=SHARE), :]
    pack_y(bufs1)
    pack_z(bufs1)

    loads[0].wait()
    dec = norm_rows(dec_v[...], qg_ref[...]).astype(BF)
    loads[1].wait()
    tokens = pl.ds(pl.multiple_of(sec * QROWS, QROWS), QROWS)
    qg[tokens, 0:WIDTH] = dot(dec, wq_v[...]).astype(BF)
    loads[2].wait()
    loads[3].wait()
    qg[tokens, WIDTH : 2 * WIDTH] = dot_t(og_v[...], mix_v[...]).astype(BF)

    pl.semaphore_wait(barrier, len(z_peers) + len(y_peers) + 5)

    parts = ((0, QROWS // 2), (QROWS // 2, QROWS // 4), (3 * QROWS // 4, QROWS // 4))

    def rows_of(s, part=None):
        first, count = (0, QROWS) if part is None else parts[part]
        return qg.at[pl.ds(pl.multiple_of(s * QROWS + first, QROWS // 4), count), :]

    def forward(s, part, recv_sem, to):
        ref = rows_of(s, part)
        remote(ref, ref, qg_s, recv_sem, to, me).start()

    def arrived(count, recv_sem):
        ref = qg.at[pl.ds(0, count), :]
        remote(ref, ref, qg_s, recv_sem, dpeer, me).wait_recv()

    def along_x(s, part, i):
        for to in (right, left, across):
            forward(s, part, x_r.at[i], to)

    spread(bufs1[0], bufs1[1], yl, y_peers, rs_sems, 0)
    spread(bufs1[4], bufs1[5], zi, z_peers, rs_sems, 4)
    forward(sec, 0, y_r.at[0], ypeer)
    along_x(sec, None, 0)
    forward(sec, None, d_r.at[0], dpeer)

    reduce_turn(bufs1, rs_sems)
    forward(sec, 1, y_r.at[1], ypeer)
    arrived(parts[0][1], y_r.at[0])
    along_x(ypeer, 0, 1)
    forward(ypeer, 0, d_r.at[1], dpeer)
    reduce_last(bufs1, rs_sems)
    rows = (own[...] + res[...]).reshape(SHARE, CHUNKS, 128)
    mean = jnp.sum(jnp.sum(rows * rows, axis=2, keepdims=True), axis=1, keepdims=True) * (1.0 / D)
    rows = rows * lax.rsqrt(mean + 1e-06) * fg_ref[...].reshape(1, CHUNKS, 128)
    own[...] = rows.reshape(PIECE, 128)
    gath_a[yl, zi] = own[:HEAD].astype(BF)
    gath_b[zi, yl] = own[HEAD:].astype(BF)
    for _, m in y_peers:
        post(gath_b.at[zi, yl], gath_b.at[zi, yl], ag_sems, 4, m)
    for _, m in z_peers:
        post(gath_a.at[yl, zi], gath_a.at[yl, zi], ag_sems, 0, m)
    forward(sec, 2, y_r.at[2], ypeer)
    for r in range(SHARE):
        for c in range(CHUNKS):
            outs[0, r : r + 1, c * 128 : (c + 1) * 128] = own[
                r * CHUNKS + c : r * CHUNKS + c + 1, :
            ].astype(BF)

    all_of(gath_b.at[zi], gath_b.at[zi], ag_sems, 4, YS - 1).wait_recv()
    for _, m in z_peers:
        post(gath_b.at[zi], gath_b.at[zi], ag_sems, 6, m)
    arrived(parts[1][1], y_r.at[1])
    along_x(ypeer, 1, 2)
    forward(ypeer, 1, d_r.at[1], dpeer)
    def far_on(part):
        arrived(3 * parts[part][1], x_r.at[part + 1])
        for dx in (3, 1, 2):
            forward(section_of(dx, 1, 0), part, d_r.at[1], dpeer)

    all_of(gath_a.at[yl], gath_a.at[yl], ag_sems, 0, ZS - 1).wait_recv()
    for _, m in y_peers:
        post(gath_a.at[yl], gath_a.at[yl], ag_sems, 2, m)
    arrived(3 * QROWS, x_r.at[0])
    for dx in (3, 1, 2):
        forward(section_of(dx, 0, 0), None, d_r.at[0], dpeer)
    arrived(parts[2][1], y_r.at[2])
    along_x(ypeer, 2, 3)
    forward(ypeer, 2, d_r.at[1], dpeer)

    far_on(0)

    def memory_rows(r, piece, line):
        for z in range(ZS):
            for y in range(YS):
                at = (z * YS + y) * PIECE + r * CHUNKS
                stage[at : at + CHUNKS] = piece(z, y)[line : line + CHUNKS].astype(F32)
        for c in range(CHUNKS):
            mem[r * MP : (r + 1) * MP, c * 128 : (c + 1) * 128] = stage[
                pl.ds(r * CHUNKS + c, MP, stride=PIECE), :
            ].astype(BF)

    all_of(gath_b, gath_b, ag_sems, 6, ZS - 1).wait_recv()
    memory_rows(2, lambda z, y: gath_b[z, y], 0)
    all_of(gath_a, gath_a, ag_sems, 2, YS - 1).wait_recv()
    for r in range(2):
        memory_rows(r, lambda z, y: gath_a[y, z], r * CHUNKS)
    loads[4].wait()
    keys = dot(mem[...], wk_v[...]).astype(BF)
    loads[5].wait()
    vals = dot(mem[...], wv_v[...]).astype(BF)

    def block(b):
        row = pl.ds(b, 1)
        for h in range(2):
            for q in range(BLOCK // TILE):
                at = pl.ds(pl.multiple_of(b * BLOCK + q * TILE, TILE), TILE)
                cols = slice(q * TILE, (q + 1) * TILE)
                s = dot_t(keys[:, h * DK : (h + 1) * DK], qg[at, h * DK : (h + 1) * DK])
                s = s * (SCALE * LOG2E)
                pg = dot_t(
                    vals[:, h * DK : (h + 1) * DK], qg[at, WIDTH + h * DK : WIDTH + (h + 1) * DK]
                )
                top = jnp.max(s, axis=0, keepdims=True)
                w = jnp.exp2(s - top)
                wts[h, b, :, cols] = w
                pgr[h, b, :, cols] = pg
                total = jnp.sum(w, axis=0, keepdims=True)
                tops[h, row, cols] = top
                stats[h, 0, row, cols] = top + jnp.log(total) * LOG2E
                stats[h, 1, row, cols] = jnp.sum(w * pg, axis=0, keepdims=True) / total

    far_on(1)
    far_on(2)
    arrived(4 * QROWS, d_r.at[0])
    for dx in (0, 3, 1, 2):
        block(section_of(dx, 0, 0) // 2)
    arrived(4 * QROWS, d_r.at[1])
    for dx in (0, 3, 1, 2):
        block(section_of(dx, 1, 0) // 2)

    def both(ref):
        return ref[0], ref[1]

    def put(ref, values):
        for i in range(2):
            ref[i] = values[i]

    sd = remote(stats.at[1 - core], got_d, st_s, sd_r, dpeer, me)
    sd.start()
    sd.wait_recv()
    put(mid, merge(both(stats.at[core]), both(got_d)))
    sy = remote(mid, got_y, st_s, sy_r, ypeer, me)
    sy.start()
    sy.wait_recv()
    put(pair, merge(both(mid), both(got_y)))
    for i, to in enumerate((across, right, left)):
        remote(pair, got_x.at[i], sx_s, sx_r, to, me).start()
    sx = remote(got_x, got_x, sx_s, sx_r, across, me)
    sx.wait_recv()
    total = merge(both(pair), both(got_x.at[1]))
    total = merge(total, both(got_x.at[2]))
    put(fin.at[core], merge(total, both(got_x.at[0])))
    sf = remote(fin.at[core], fin.at[core], st_s, sf_r, dpeer, me)
    sf.start()

    def gradients(h):
        lanes = pl.ds(pl.multiple_of(h * DK, DK), DK)
        grad_lanes = pl.ds(pl.multiple_of(WIDTH + h * DK, DK), DK)

        def one(b, carry):
            at = pl.ds(pl.multiple_of(b * BLOCK, BLOCK), BLOCK)
            row = pl.ds(b, 1)
            factor = jnp.exp2(tops[h, row, :] - fin[h, 0, row, :])
            delta = fin[h, 1, row, :]
            probs = wts[h, b] * factor
            sg = (probs * (pgr[h, b] - delta) * SCALE).astype(BF)
            kg = carry[0] + dot(sg, qg[at, lanes])
            vg = carry[1] + dot(probs.astype(BF), qg[at, grad_lanes])
            return kg, vg

        zero = jnp.zeros((ROWS, DK), F32)
        kg, vg = lax.fori_loop(0, BLOCKS, one, (zero, zero), unroll=True)
        grads[0, :, lanes] = kg.astype(BF)
        grads[1, :, lanes] = vg.astype(BF)

    gradients(core)
    sf.wait_recv()
    gradients(1 - core)
    def partial_rows(first, last):
        low, high = first * MP, last * MP
        part = dot_t(grads[0, low:high], wk_v[...]) + dot_t(grads[1, low:high], wv_v[...])
        for r in range(first, last):
            for c in range(CHUNKS):
                stage[pl.ds(r * CHUNKS + c, MP, stride=PIECE), :] = part[
                    (r - first) * MP : (r - first + 1) * MP, c * 128 : (c + 1) * 128
                ]

    partial_rows(0, 2)
    pack_y(bufs2)
    spread(bufs2[0], bufs2[1], yl, y_peers, rs2_sems, 0)
    partial_rows(2, 3)
    pack_z(bufs2)
    spread(bufs2[4], bufs2[5], zi, z_peers, rs2_sems, 4)
    reduce_turn(bufs2, rs2_sems)
    reduce_last(bufs2, rs2_sems)

    for copy in started:
        copy.wait_send()
    sent = qg.at[pl.ds(0, 15 * QROWS), :]
    remote(sent, sent, qg_s, d_r.at[0], dpeer, me).wait_send()
    sx.wait_send()
    remote(got_x, got_x, st_s, sx_r, dpeer, me).wait_send()
    for r in range(SHARE):
        for c in range(CHUNKS):
            outs[1, r : r + 1, c * 128 : (c + 1) * 128] = own[
                r * CHUNKS + c : r * CHUNKS + c + 1, :
            ].astype(BF)


def body(
    encoder_input, input_gain, expand_weight, reduce_weight, final_gain, decoder_input, query_gain,
    query_weight, key_weight, value_weight, mixing_weight, output_gradient,
):
    vmem = pl.BlockSpec(memory_space=pltpu.VMEM)
    hbm = pl.BlockSpec(memory_space=pl.ANY)
    dma = pltpu.SemaphoreType.DMA
    piece2 = (2, BLOCKS, BLOCK)

    def sums_at_owner(head):
        tail = PIECE - head
        shapes = (
            (YS, ZS, head, 128), (YS, ZS, head, 128), (ZS, head, 128), (ZS, head, 128),
            (ZS, YS, tail, 128), (ZS, YS, tail, 128), (YS, tail, 128), (YS, tail, 128),
        )
        return [pltpu.VMEM(shape, BF) for shape in shapes]

    outs = pl.pallas_call(
        kernel,
        out_shape=pltpu.VMEM((2, SHARE, D), BF),
        in_specs=[hbm, vmem, hbm, hbm, vmem, hbm, vmem, hbm, hbm, hbm, hbm, hbm],
        out_specs=vmem,
        scratch_shapes=[
            pltpu.VMEM(encoder_input.shape, BF),
            pltpu.VMEM(expand_weight.shape, BF),
            pltpu.VMEM(reduce_weight.shape, BF),
            pltpu.VMEM(decoder_input.shape, BF),
            pltpu.VMEM(query_weight.shape, BF),
            pltpu.VMEM(key_weight.shape, BF),
            pltpu.VMEM(value_weight.shape, BF),
            pltpu.VMEM(mixing_weight.shape, BF),
            pltpu.VMEM(output_gradient.shape, BF),
            dma((9,)),
            pltpu.VMEM((CHUNKS, ROWS, 128), F32),
            pltpu.VMEM((MP * PIECE, 128), F32),
            pltpu.VMEM((PIECE, 128), F32),
            pltpu.VMEM((PIECE, 128), F32),
            sums_at_owner(1 * CHUNKS),
            sums_at_owner(2 * CHUNKS),
            pltpu.VMEM((YS, ZS, HEAD, 128), BF),
            pltpu.VMEM((ZS, YS, TAIL, 128), BF),
            pltpu.VMEM((ROWS, D), BF),
            pltpu.VMEM((QALL, 2 * WIDTH), BF),
            pltpu.VMEM((2, BLOCKS, ROWS, BLOCK), F32),
            pltpu.VMEM((2, BLOCKS, ROWS, BLOCK), F32),
            pltpu.VMEM((2, BLOCKS, BLOCK), F32),
            pltpu.VMEM((2, *piece2), F32),
            pltpu.VMEM(piece2, F32),
            pltpu.VMEM(piece2, F32),
            pltpu.VMEM(piece2, F32),
            pltpu.VMEM(piece2, F32),
            pltpu.VMEM((3, *piece2), F32),
            pltpu.VMEM((2, *piece2), F32),
            pltpu.VMEM((2, ROWS, WIDTH), BF),
            dma((8,)), dma((8,)), dma((8,)),
            dma, dma((3,)), dma((4,)), dma((2,)), dma, dma, dma, dma, dma, dma,
        ],
        compiler_params=pltpu.CompilerParams(
            collective_id=0, has_side_effects=True, vmem_limit_bytes=60 * 1024 * 1024
        ),
    )(
        encoder_input, input_gain.reshape(1, D), expand_weight, reduce_weight,
        final_gain.reshape(CHUNKS, 128), decoder_input, query_gain.reshape(1, D), query_weight,
        key_weight, value_weight, mixing_weight, output_gradient,
    )
    return outs[0], outs[1]


def solution(mesh):
    in_specs = (
        P("section", None), P(), P(None, "mp"), P("mp", None), P(), P("section", None), P(),
        P(None, "mp"), P(None, "mp"), P(None, "mp"), P("mp", None), P("section", None),
    )
    out_specs = (P(("section", "mp"), None), P(("section", "mp"), None))
    return jax.shard_map(body, mesh=mesh, in_specs=in_specs, out_specs=out_specs, check_vma=False)
```

time: 81.3 us -> 74.5 us (0.916)
  Pallas kernels: 77.6 us -> 72.2 us
  local copies, waits for them, and re-layouts: 2.6 us -> 0.61 us
    pallas_call x1, Pallas kernels: 77.6 us -> 72.2 us  [body(): pl.pallas_call(kernel, out_shape=pltpu.VMEM((2, SHARE, D), BF), in_specs=...]
    unnamed x2 -> x0, local copies, waits for them, and re-layouts: 2.6 us -> none
where the time goes in v3:
time: 74.5 us; the launch traced here: 73.5 us
  Pallas kernels  72.2 us (97%)
    pallas_call x1, Pallas kernels, body(): pl.pallas_call(kernel, out_shape=pltpu.VMEM((2, SHARE, D), BF), in_specs=...  72.2 us

profile of v3, /device:TPU:1, one launch (start us, length us, event | category | flops | bytes accessed | tf_op | source)
XLA Modules:
  0.0 73.5 jit_solution(10086921442440802184)
XLA Ops:
  0.6 72.2 %shard_map.131 = bf16[2,3,1024]{2,1,0:T(4,128)(2,1)S(1)} custom-call(bf16[144,1024]{1,0:T(8,128)(2,1)} %x_hbm.1, f32[1,1024]{1,0:T(1,128)} %bitcast.7, bf16[1024,1024]{1,0:T(8,128)(2,1)} %we_hbm.1, bf16[1024,1024]{1,0:T(8,128)(2,1)} %wr_hbm.1, f32[8,128]{1,0:T(8,128)} %bitcast.8, bf16[256,1024]{1,0:T(8,128)(2,1)} %dec_hbm.1, f32[1,1024]{1,0:T(1,128)} %bitcast.9, ...), custom_call_target="tpu_custom_call" | custom-call | tf_op jit(solution)/shard_map/pallas_call | solution.py:407
  72.9 0.6 slice_bitcast_fusion

commit v4 on v3

--- a/solution.py
+++ b/solution.py
@@ -189,11 +189,11 @@
 
     pl.semaphore_wait(barrier, len(z_peers) + len(y_peers) + 5)
 
-    parts = ((0, QROWS // 2), (QROWS // 2, QROWS // 4), (3 * QROWS // 4, QROWS // 4))
+    parts = ((0, 112), (112, 80), (192, 64), (0, 128), (128, 128))
 
     def rows_of(s, part=None):
         first, count = (0, QROWS) if part is None else parts[part]
-        return qg.at[pl.ds(pl.multiple_of(s * QROWS + first, QROWS // 4), count), :]
+        return qg.at[pl.ds(pl.multiple_of(s * QROWS + first, 16), count), :]
 
     def forward(s, part, recv_sem, to):
         ref = rows_of(s, part)
@@ -210,11 +210,17 @@
     spread(bufs1[0], bufs1[1], yl, y_peers, rs_sems, 0)
     spread(bufs1[4], bufs1[5], zi, z_peers, rs_sems, 4)
     forward(sec, 0, y_r.at[0], ypeer)
-    along_x(sec, None, 0)
+    for to in (right, left):
+        forward(sec, None, x_r.at[0], to)
     forward(sec, None, d_r.at[0], dpeer)
 
     reduce_turn(bufs1, rs_sems)
     forward(sec, 1, y_r.at[1], ypeer)
+    arrived(2 * QROWS, x_r.at[0])
+    forward(left, 3, x_r.at[4], right)
+    forward(right, 4, x_r.at[4], left)
+    for s in (left, right):
+        forward(s, None, d_r.at[0], dpeer)
     arrived(parts[0][1], y_r.at[0])
     along_x(ypeer, 0, 1)
     forward(ypeer, 0, d_r.at[1], dpeer)
@@ -250,9 +256,8 @@
     all_of(gath_a.at[yl], gath_a.at[yl], ag_sems, 0, ZS - 1).wait_recv()
     for _, m in y_peers:
         post(gath_a.at[yl], gath_a.at[yl], ag_sems, 2, m)
-    arrived(3 * QROWS, x_r.at[0])
-    for dx in (3, 1, 2):
-        forward(section_of(dx, 0, 0), None, d_r.at[0], dpeer)
+    arrived(QROWS, x_r.at[4])
+    forward(across, None, d_r.at[0], dpeer)
     arrived(parts[2][1], y_r.at[2])
     along_x(ypeer, 2, 3)
     forward(ypeer, 2, d_r.at[1], dpeer)
@@ -271,6 +276,7 @@
 
     all_of(gath_b, gath_b, ag_sems, 6, ZS - 1).wait_recv()
     memory_rows(2, lambda z, y: gath_b[z, y], 0)
+    far_on(1)
     all_of(gath_a, gath_a, ag_sems, 2, YS - 1).wait_recv()
     for r in range(2):
         memory_rows(r, lambda z, y: gath_a[y, z], r * CHUNKS)
@@ -299,7 +305,6 @@
                 stats[h, 0, row, cols] = top + jnp.log(total) * LOG2E
                 stats[h, 1, row, cols] = jnp.sum(w * pg, axis=0, keepdims=True) / total
 
-    far_on(1)
     far_on(2)
     arrived(4 * QROWS, d_r.at[0])
     for dx in (0, 3, 1, 2):
@@ -442,7 +447,7 @@
             pltpu.VMEM((2, *piece2), F32),
             pltpu.VMEM((2, ROWS, WIDTH), BF),
             dma((8,)), dma((8,)), dma((8,)),
-            dma, dma((3,)), dma((4,)), dma((2,)), dma, dma, dma, dma, dma, dma,
+            dma, dma((3,)), dma((5,)), dma((2,)), dma, dma, dma, dma, dma, dma,
         ],
         compiler_params=pltpu.CompilerParams(
             collective_id=0, has_side_effects=True, vmem_limit_bytes=60 * 1024 * 1024

time: 74.5 us -> 73.2 us (0.983)
  no operation moved by 1% of the time
where the time goes in v4:
time: 73.2 us; the launch traced here: 72.8 us
  Pallas kernels  71.5 us (98%)
    pallas_call x1, Pallas kernels, body(): pl.pallas_call(kernel, out_shape=pltpu.VMEM((2, SHARE, D), BF), in_specs=...  71.5 us

profile of v4, /device:TPU:1, one launch (start us, length us, event | category | flops | bytes accessed | tf_op | source)
XLA Modules:
  0.0 72.8 jit_solution(17103521632598217469)
XLA Ops:
  0.6 71.5 %shard_map.131 = bf16[2,3,1024]{2,1,0:T(4,128)(2,1)S(1)} custom-call(bf16[144,1024]{1,0:T(8,128)(2,1)} %x_hbm.1, f32[1,1024]{1,0:T(1,128)} %bitcast.7, bf16[1024,1024]{1,0:T(8,128)(2,1)} %we_hbm.1, bf16[1024,1024]{1,0:T(8,128)(2,1)} %wr_hbm.1, f32[8,128]{1,0:T(8,128)} %bitcast.8, bf16[256,1024]{1,0:T(8,128)(2,1)} %dec_hbm.1, f32[1,1024]{1,0:T(1,128)} %bitcast.9, ...), custom_call_target="tpu_custom_call" | custom-call | tf_op jit(solution)/shard_map/pallas_call | solution.py:412
  72.2 0.6 slice_bitcast_fusion
